TPU v7x, 32 devices: a whole 2x2x4 slice. The times are simulated.
32 devices in a mesh: gz: 2 (over core), row: 4 (over y, x), col: 4 (over z).
Axes of the slice: x: 2, y: 2, z: 4, core: 2. Of those that a mesh axis runs over, the one named last changes fastest.
Arguments:
- right_sides: float32 [32, 4, 16, 256], P(('gz', 'row', 'col')), may hold values from -6 to 6
- lower_inverse: bfloat16 [32, 4, 256, 256], P(('gz', 'row', 'col')), may hold values from -0.375 to 0.375
- upper_inverse: bfloat16 [32, 4, 256, 256], P(('gz', 'row', 'col')), may hold values from -0.375 to 0.375
- lower_blocks: bfloat16 [32, 4, 2, 256, 256], P(('gz', 'row', 'col')), may hold values from -0.125 to 0.125
- upper_blocks: bfloat16 [32, 4, 2, 256, 256], P(('gz', 'row', 'col')), may hold values from -0.125 to 0.125
- node_widths: int32 [32, 4], P(('gz', 'row', 'col')), may hold values from 128 to 256, as said below
- far_levels: int32 [32, 4], P(('gz', 'row', 'col')), may hold values from 0 to 5, as said below
- owner_level: int32 [32], replicated, may hold values from 0 to 5, as said below
Outputs:
- solution: float32 [32, 4, 16, 256], P(('gz', 'row', 'col'))
Inputs may be any that keep to these rules, and one draw needn't show every extreme that they name: Columns c >= node_widths of a supernode are padding; every device holds a supernode with all 256 columns. `far_levels`: between 2 and 5 where the supernode has two or more ancestors, but never past the root; 1 where it has one; 0 for the root and for the slot of the device that owns no separator. `owner_level`: every separator of level u is owned by exactly one device of its group (the devices t with the same t // 2**u); one device owns none and holds 0.
All inputs are finite; a program needn't handle non-finite values.
Results may differ from a plain program's by a relative error of at most 0.018.
Values may be sent and summed in bfloat16 or wider, within the bound.
A program may use at most 64 MiB of HBM per device.

v0:
```python
import jax
import jax.numpy as jnp
from jax import lax
from jax.sharding import PartitionSpec as P

W = 256
RHS = 16
NB = 2
LOCAL_LEVELS = 2
LOCAL_COUNT = 3


def level_start(height):
    return 2**LOCAL_LEVELS - 2 ** (LOCAL_LEVELS - height)


def apply_blocks(vectors, blocks):
    return jnp.einsum("snrk,snak->snra", vectors, blocks, preferred_element_type=jnp.float32)


def apply_single(vectors, blocks):
    return jnp.einsum("srk,sak->sra", vectors, blocks, preferred_element_type=jnp.float32)


def forward_local(right_sides, lower_inverse, lower_blocks, padding, far_levels, upper_levels):
    batch_size = right_sides.shape[0]
    pending = jnp.zeros((batch_size, LOCAL_COUNT, RHS, W), jnp.float32)
    upper_pending = jnp.zeros((batch_size, upper_levels, RHS, W), jnp.float32)
    solved = []
    for height in range(LOCAL_LEVELS):
        offset = level_start(height)
        amount = 2 ** (LOCAL_LEVELS - 1 - height)
        residue = (
            right_sides[:, offset : offset + amount] - pending[:, offset : offset + amount]
        ).astype(jnp.bfloat16)
        solved_now = padding[:, offset : offset + amount] * apply_blocks(
            residue, lower_inverse[:, offset : offset + amount]
        )
        solved.append(solved_now)
        rounded = solved_now.astype(jnp.bfloat16)
        for block_id in range(NB):
            product = apply_blocks(rounded, lower_blocks[:, offset : offset + amount, block_id])
            for distance in range(1, upper_levels + 1):
                if block_id == 0 and distance > 1:
                    continue
                if block_id == 0:
                    chosen = product
                else:
                    matches = far_levels[:, offset : offset + amount] == distance
                    chosen = jnp.where(matches[:, :, None, None], product, 0.0)
                target = height + distance
                if target < LOCAL_LEVELS:
                    target_count = amount // 2**distance
                    folded = chosen.reshape(batch_size, target_count, 2**distance, RHS, W).sum(
                        axis=2
                    )
                    begin_at = level_start(target)
                    pending = pending.at[:, begin_at : begin_at + target_count].add(folded)
                else:
                    upper_pending = upper_pending.at[:, target - LOCAL_LEVELS].add(
                        chosen.sum(axis=1)
                    )
    return (jnp.concatenate(solved, axis=1), upper_pending)


def backward_local(forward, upper_inverse, upper_blocks, padding, far_levels, upper_known):
    upper_levels = upper_known.shape[1]
    solutions = [None] * LOCAL_LEVELS
    for height in reversed(range(LOCAL_LEVELS)):
        offset = level_start(height)
        amount = 2 ** (LOCAL_LEVELS - 1 - height)
        residue = forward[:, offset : offset + amount]
        for block_id in range(NB):
            operand = jnp.zeros(residue.shape, jnp.float32)
            for distance in range(1, upper_levels + 1):
                if block_id == 0 and distance > 1:
                    continue
                target = height + distance
                if target < LOCAL_LEVELS:
                    known_part = jnp.repeat(solutions[target], 2**distance, axis=1)
                else:
                    known_part = jnp.broadcast_to(
                        upper_known[:, target - LOCAL_LEVELS][:, None], residue.shape
                    )
                if block_id == 0:
                    operand = known_part
                else:
                    matches = far_levels[:, offset : offset + amount] == distance
                    operand = operand + jnp.where(matches[:, :, None, None], known_part, 0.0)
            residue = residue - apply_blocks(
                operand.astype(jnp.bfloat16), upper_blocks[:, offset : offset + amount, block_id]
            )
        solutions[height] = padding[:, offset : offset + amount] * apply_blocks(
            residue.astype(jnp.bfloat16), upper_inverse[:, offset : offset + amount]
        )
    return jnp.concatenate(solutions, axis=1)


def spread_slots(partial_value, slot_count, slot_at):
    chosen = (jnp.arange(slot_count, dtype=jnp.int32) == slot_at)[:, None, None]
    return jnp.where(chosen, partial_value, 0.0)


def group_total(partial_value, height, layout, places):
    col_levels, grid_levels, col_span, grid_span, total_span = layout
    if height <= col_levels:
        slot_at = places[0] // 2**height
        summed = lax.psum(
            spread_slots(partial_value, col_span // 2**height, slot_at).astype(jnp.bfloat16), "col"
        ).astype(jnp.float32)
    elif height <= grid_levels:
        slot_at = places[1] // 2**height
        summed = lax.psum(
            spread_slots(partial_value, grid_span // 2**height, slot_at), ("row", "col")
        )
    else:
        slot_at = places[2] // 2**height
        summed = lax.psum(
            spread_slots(partial_value, total_span // 2**height, slot_at), ("gz", "row", "col")
        )
    return lax.dynamic_index_in_dim(summed, slot_at, 0, keepdims=True)


def group_share(partial_value, height, layout, places):
    col_levels, grid_levels, col_span, grid_span, total_span = layout
    if height <= col_levels:
        slot_at = places[0] // 2**height
        summed = lax.psum(
            spread_slots(partial_value, col_span // 2**height, slot_at).astype(jnp.bfloat16), "col"
        ).astype(jnp.float32)
    elif height <= grid_levels:
        slot_at = places[1] // 2**height
        summed = lax.psum(
            spread_slots(partial_value, grid_span // 2**height, slot_at), ("row", "col")
        )
    else:
        slot_at = places[2] // 2**height
        summed = lax.psum(
            spread_slots(partial_value, total_span // 2**height, slot_at), ("gz", "row", "col")
        )
    return lax.dynamic_index_in_dim(summed, slot_at, 0, keepdims=True)


def local(
    right_sides,
    lower_inverse,
    upper_inverse,
    lower_blocks,
    upper_blocks,
    node_widths,
    far_levels,
    owner_level,
):
    col_span = lax.axis_size("col")
    row_span = lax.axis_size("row")
    layer_span = lax.axis_size("gz")
    col_levels = col_span.bit_length() - 1
    grid_levels = col_levels + row_span.bit_length() - 1
    upper_levels = grid_levels + layer_span.bit_length() - 1
    col_place = lax.axis_index("col")
    grid_place = lax.axis_index("row") * col_span + col_place
    device = lax.axis_index("gz") * row_span * col_span + grid_place
    layout = (
        col_levels,
        grid_levels,
        col_span,
        row_span * col_span,
        layer_span * row_span * col_span,
    )
    places = (col_place, grid_place, device)
    columns = jnp.arange(W, dtype=jnp.int32)
    padding = (columns[None, None, None, :] < node_widths[:, :, None, None]).astype(jnp.float32)
    forward_nodes, upper_pending = forward_local(
        right_sides[:, :LOCAL_COUNT],
        lower_inverse[:, :LOCAL_COUNT],
        lower_blocks[:, :LOCAL_COUNT],
        padding[:, :LOCAL_COUNT],
        far_levels[:, :LOCAL_COUNT],
        upper_levels,
    )
    own_rights = right_sides[:, LOCAL_COUNT]
    own_padding = padding[:, LOCAL_COUNT]
    own_far = far_levels[:, LOCAL_COUNT]
    my_level = lax.dynamic_index_in_dim(owner_level, device, 0, keepdims=False)
    own_forward = jnp.zeros((1, RHS, W), jnp.float32)
    for height in range(1, upper_levels + 1):
        gathered = group_total(upper_pending[:, height - 1], height, layout, places)
        owner_here = my_level == height
        residue = (own_rights - gathered).astype(jnp.bfloat16)
        solved_now = jnp.where(
            owner_here, own_padding * apply_single(residue, lower_inverse[:, LOCAL_COUNT]), 0.0
        )
        own_forward = own_forward + solved_now
        rounded = solved_now.astype(jnp.bfloat16)
        for block_id in range(NB):
            product = apply_single(rounded, lower_blocks[:, LOCAL_COUNT, block_id])
            for distance in range(1, upper_levels + 1):
                if block_id == 0 and distance > 1:
                    continue
                target = height + distance
                if target > upper_levels:
                    continue
                if block_id == 0:
                    chosen = product
                else:
                    chosen = jnp.where((own_far == distance)[:, None, None], product, 0.0)
                upper_pending = upper_pending.at[:, target - 1].add(chosen)
    upper_known = jnp.zeros((1, upper_levels, RHS, W), jnp.float32)
    own_solution = jnp.zeros((1, RHS, W), jnp.float32)
    for height in range(upper_levels, 0, -1):
        owner_here = my_level == height
        residue = own_forward
        for block_id in range(NB):
            operand = jnp.zeros((1, RHS, W), jnp.float32)
            for distance in range(1, upper_levels + 1):
                if block_id == 0 and distance > 1:
                    continue
                target = height + distance
                if target > upper_levels:
                    continue
                known_part = upper_known[:, target - 1]
                if block_id == 0:
                    operand = known_part
                else:
                    operand = operand + jnp.where(
                        (own_far == distance)[:, None, None], known_part, 0.0
                    )
            residue = residue - apply_single(
                operand.astype(jnp.bfloat16), upper_blocks[:, LOCAL_COUNT, block_id]
            )
        solved_now = jnp.where(
            owner_here,
            own_padding * apply_single(residue.astype(jnp.bfloat16), upper_inverse[:, LOCAL_COUNT]),
            0.0,
        )
        own_solution = own_solution + solved_now
        shared = group_share(solved_now, height, layout, places)
        upper_known = upper_known.at[:, height - 1].set(shared)
    local_solution = backward_local(
        forward_nodes,
        upper_inverse[:, :LOCAL_COUNT],
        upper_blocks[:, :LOCAL_COUNT],
        padding[:, :LOCAL_COUNT],
        far_levels[:, :LOCAL_COUNT],
        upper_known,
    )
    return jnp.concatenate([local_solution, own_solution[:, None]], axis=1)


def solution(mesh):
    return jax.shard_map(
        local,
        mesh=mesh,
        in_specs=(
            P(("gz", "row", "col"), None, None, None),
            P(("gz", "row", "col"), None, None, None),
            P(("gz", "row", "col"), None, None, None),
            P(("gz", "row", "col"), None, None, None, None),
            P(("gz", "row", "col"), None, None, None, None),
            P(("gz", "row", "col"), None),
            P(("gz", "row", "col"), None),
            P(),
        ),
        out_specs=P(("gz", "row", "col"), None, None, None),
        check_vma=False,
    )
```

profile of v0, /device:TPU:0, one launch (start us, length us, event | category | flops | bytes accessed | tf_op | source)
XLA Modules:
  0.0 453.6 jit_solution(13407759819667578866)
XLA Ops:
  0.0 0.7 compare_bitcast_fusion.3
  0.8 0.7 fusion.307
  1.5 1.1 convolution_multiply_fusion.1
  2.6 1.2 select_reduce_fusion.4
  3.9 1.4 convolution_multiply_fusion.13
  5.3 0.2 fusion.24
  5.5 0.7 copy-done.5
  6.1 0.6 fusion.324
  7.4 0.2 fusion.167
  10.2 20.5 %psum.70 = bf16[2,16,256]{2,1,0:T(8,128)(2,1)S(1)} all-reduce(bf16[2,16,256]{2,1,0:T(8,128)(2,1)S(1)} %select_convert_fusion.1), channel_id=1, replica_groups=mesh['gz'=2,'row'=4,'col'=4] {'col'}, use_global_device_ids=true, to_apply=%region_5.6 | all-reduce | flops 8192 | bytes 32768 | tf_op jit(solution)/shard_map/psum | solution.py:108
  30.7 0.7 copy-done.6
  31.4 0.6 dynamic_slice.24
  32.7 0.2 fusion.23
  32.8 0.2 fusion.22
  33.7 0.2 fusion.166
  35.9 8.5 %psum.71 = bf16[1,16,256]{2,1,0:T(8,128)(2,1)S(1)} all-reduce(bf16[1,16,256]{2,1,0:T(8,128)(2,1)S(1)} %fusion.218), channel_id=1, replica_groups=mesh['gz'=2,'row'=4,'col'=4] {'col'}, use_global_device_ids=true, to_apply=%region_6.7 | all-reduce | flops 4096 | bytes 16384 | tf_op jit(solution)/shard_map/psum | solution.py:108
  45.1 0.2 fusion.21
  45.2 0.2 fusion.20
  45.4 0.2 fusion.165
  45.8 75.8 %psum.72 = f32[2,16,256]{2,1,0:T(8,128)S(1)} all-reduce(f32[2,16,256]{2,1,0:T(8,128)S(1)} %broadcast_select_fusion.1), channel_id=1, replica_groups=mesh['gz'=2,'row'=4,'col'=4] {'row','col'}, use_global_device_ids=true, to_apply=%region_7.8 | all-reduce | flops 8192 | bytes 65536 | tf_op jit(solution)/shard_map/psum | solution.py:113
  122.3 0.2 fusion.19
  122.4 0.2 fusion.78
  122.6 0.2 fusion.18
  122.8 72.1 %psum.73 = f32[1,16,256]{2,1,0:T(8,128)S(1)} all-reduce(f32[1,16,256]{2,1,0:T(8,128)S(1)} %fusion.18), channel_id=1, replica_groups=mesh['gz'=2,'row'=4,'col'=4] {'row','col'}, use_global_device_ids=true, to_apply=%region_8.9 | all-reduce | flops 4096 | bytes 32768 | tf_op jit(solution)/shard_map/psum | solution.py:113
  195.5 0.2 fusion.14
  195.7 0.2 fusion.13
  195.9 0.2 fusion.12
  196.0 36.9 %psum.74 = f32[1,16,256]{2,1,0:T(8,128)S(1)} all-reduce(f32[1,16,256]{2,1,0:T(8,128)S(1)} %fusion.12), channel_id=1, replica_groups=mesh['gz'=2,'row'=4,'col'=4] {'gz','row','col'}, use_global_device_ids=true, to_apply=%region_9.10 | all-reduce | flops 4096 | bytes 32768 | tf_op jit(solution)/shard_map/psum | solution.py:118
  233.6 0.2 fusion.8
  233.7 0.2 convolution_subtract_fusion.13
  233.9 0.3 fusion.6
  234.3 41.4 %psum.75 = f32[1,16,256]{2,1,0:T(8,128)S(1)} all-reduce(f32[1,16,256]{2,1,0:T(8,128)S(1)} %select_bitcast_fusion.1), channel_id=1, replica_groups=mesh['gz'=2,'row'=4,'col'=4] {'gz','row','col'}, use_global_device_ids=true, to_apply=%region_10.11 | all-reduce | flops 4096 | bytes 32768 | tf_op jit(solution)/shard_map/psum | solution.py:138
  275.7 0.1 convolution_subtract_fusion.11
  275.9 0.3 fusion.5
  276.2 76.1 %psum.76 = f32[1,16,256]{2,1,0:T(8,128)S(1)} all-reduce(f32[1,16,256]{2,1,0:T(8,128)S(1)} %select_bitcast_fusion), channel_id=1, replica_groups=mesh['gz'=2,'row'=4,'col'=4] {'row','col'}, use_global_device_ids=true, to_apply=%region_11.12 | all-reduce | flops 4096 | bytes 32768 | tf_op jit(solution)/shard_map/psum | solution.py:133
  352.3 0.1 convolution_subtract_fusion.9
  352.5 0.3 fusion.4
  352.9 72.1 %psum.77 = f32[2,16,256]{2,1,0:T(8,128)S(1)} all-reduce(f32[2,16,256]{2,1,0:T(8,128)S(1)} %broadcast_select_fusion), channel_id=1, replica_groups=mesh['gz'=2,'row'=4,'col'=4] {'row','col'}, use_global_device_ids=true, to_apply=%region_12.13 | all-reduce | flops 8192 | bytes 65536 | tf_op jit(solution)/shard_map/psum | solution.py:133
  425.1 0.3 fusion.3
  425.4 8.5 %psum.78 = bf16[1,16,256]{2,1,0:T(8,128)(2,1)S(1)} all-reduce(bf16[1,16,256]{2,1,0:T(8,128)(2,1)S(1)} %fusion.201), channel_id=1, replica_groups=mesh['gz'=2,'row'=4,'col'=4] {'col'}, use_global_device_ids=true, to_apply=%region_13.14 | all-reduce | flops 4096 | bytes 16384 | tf_op jit(solution)/shard_map/psum | solution.py:128
  434.0 0.2 convolution_subtract_fusion.5
  434.1 0.3 fusion.2
  434.5 17.4 %psum.79 = bf16[2,16,256]{2,1,0:T(8,128)(2,1)S(1)} all-reduce(bf16[2,16,256]{2,1,0:T(8,128)(2,1)S(1)} %select_convert_fusion), channel_id=1, replica_groups=mesh['gz'=2,'row'=4,'col'=4] {'col'}, use_global_device_ids=true, to_apply=%region_14.15 | all-reduce | flops 8192 | bytes 32768 | tf_op jit(solution)/shard_map/psum | solution.py:128
  451.9 0.2 convolution_subtract_fusion.3
  452.1 0.3 fusion.325
  452.4 0.2 convolution_subtract_fusion.1
  452.6 0.3 fusion
  453.0 0.6 pad_maximum_fusion
  (49 shorter events, 0.7 us)
Async XLA Ops:
  0.0 5.3 %copy-start.1 = (bf16[1,4,2,256,256]{4,3,2,1,0:T(8,128)(2,1)S(1)}, bf16[1,4,2,256,256]{4,3,2,1,0:T(8,128)(2,1)}, u32[]{:S(2)}) copy-start(bf16[1,4,2,256,256]{4,3,2,1,0:T(8,128)(2,1)} %param.73) | copy-start | bytes 3145732
  3.9 28.8 %copy-start.2 = (bf16[1,4,256,256]{3,2,1,0:T(8,128)(2,1)S(1)}, bf16[1,4,256,256]{3,2,1,0:T(8,128)(2,1)}, u32[]{:S(2)}) copy-start(bf16[1,4,256,256]{3,2,1,0:T(8,128)(2,1)} %param.71) | copy-start | bytes 1572868
  5.5 0.7 copy-start.5
  10.1 22.6 %copy-start.4 = (f32[1,4,16,256]{3,2,1,0:T(8,128)S(1)}, f32[1,4,16,256]{3,2,1,0:T(8,128)}, u32[]{:S(2)}) copy-start(f32[1,4,16,256]{3,2,1,0:T(8,128)} %param.70) | copy-start | bytes 196612
  30.7 0.7 copy-start.6
  45.4 188.3 %copy-start = (bf16[1,4,2,256,256]{4,3,2,1,0:T(8,128)(2,1)S(1)}, bf16[1,4,2,256,256]{4,3,2,1,0:T(8,128)(2,1)}, u32[]{:S(2)}) copy-start(bf16[1,4,2,256,256]{4,3,2,1,0:T(8,128)(2,1)} %param.74) | copy-start | bytes 3145732
  195.5 38.4 %copy-start.3 = (bf16[1,4,256,256]{3,2,1,0:T(8,128)(2,1)S(1)}, bf16[1,4,256,256]{3,2,1,0:T(8,128)(2,1)}, u32[]{:S(2)}) copy-start(bf16[1,4,256,256]{3,2,1,0:T(8,128)(2,1)} %param.72) | copy-start | bytes 1572868
where the time goes:
time: 454 us
  blocking collectives  429 us (94%)
  matrix products  9.61 us (2%)
  between operations  9.28 us (2%)
    psum x2, blocking collectives, group_share(): lax.psum(spread_slots(partial_value, grid_span // 2 ** height, slot_at),...  148 us
    psum x2, blocking collectives, group_total(): lax.psum(spread_slots(partial_value, grid_span // 2 ** height, slot_at),...  148 us
    psum x1, blocking collectives, group_share(): lax.psum(spread_slots(partial_value, total_span // 2 ** height, slot_at),...  41.4 us
    psum x1, blocking collectives, group_total(): lax.psum(spread_slots(partial_value, total_span // 2 ** height, slot_at),...  36.9 us
    psum x2, blocking collectives, group_total(): lax.psum(spread_slots(partial_value, col_span // 2 ** height, slot_at).as...  29 us
    psum x2, blocking collectives, group_share(): lax.psum(spread_slots(partial_value, col_span // 2 ** height, slot_at).as...  25.9 us

commit v1 on v0

v1 whole, which is shorter than its diff:
```python
import functools

import jax
import jax.numpy as jnp
from jax import lax
from jax.experimental import pallas as pl
from jax.experimental.pallas import tpu as pltpu
from jax.sharding import PartitionSpec as P

W = 256
RHS = 16
NB = 2
LOCAL_LEVELS = 2
LOCAL_COUNT = 3
OWN = LOCAL_COUNT
AXES = ("gz", "row", "col")


def flip_bits(coord, mask):
    flipped = coord
    bit = 1
    while bit <= mask:
        if mask & bit:
            flipped = flipped + bit - 2 * bit * lax.rem(lax.div(coord, bit), 2)
        bit *= 2
    return flipped


def exchange_plan(level, col_levels):
    phases = []
    low = 0
    while low < level:
        high = min(low + 2, col_levels, level) if low < col_levels else min(low + 3, level)
        phases.append([step << low for step in range(1, 1 << (high - low))])
        low = high
    return phases


def times(vectors, matrix):
    return lax.dot_general(
        vectors, matrix, (((1,), (1,)), ((), ())), preferred_element_type=jnp.float32
    )


def half(values):
    return values.astype(jnp.bfloat16)


def kernel(
    spans,
    plans,
    rights_hbm,
    lower_inverse_hbm,
    upper_inverse_hbm,
    lower_blocks_hbm,
    upper_blocks_hbm,
    widths_ref,
    far_ref,
    owner_ref,
    out_ref,
    rights,
    lower_inverse,
    upper_inverse,
    lower_blocks,
    upper_blocks,
    outgoing,
    incoming,
    load_sems,
    send_sems,
    recv_sems,
):
    layer_span, row_span, col_span = spans
    upper_levels = len(plans)
    layer_at = lax.axis_index("gz")
    row_at = lax.axis_index("row")
    col_at = lax.axis_index("col")
    device = (layer_at * row_span + row_at) * col_span + col_at

    def peer(offset):
        return (
            flip_bits(layer_at, offset // (row_span * col_span)),
            flip_bits(row_at, offset // col_span % row_span),
            flip_bits(col_at, offset % col_span),
        )

    pieces = [
        (rights_hbm.at[0], rights),
        (lower_inverse_hbm.at[0, pl.ds(0, 2)], lower_inverse.at[pl.ds(0, 2)]),
        (lower_blocks_hbm.at[0, pl.ds(0, 2)], lower_blocks.at[pl.ds(0, 2)]),
        (lower_inverse_hbm.at[0, pl.ds(2, 2)], lower_inverse.at[pl.ds(2, 2)]),
        (lower_blocks_hbm.at[0, pl.ds(2, 2)], lower_blocks.at[pl.ds(2, 2)]),
        (upper_blocks_hbm.at[0], upper_blocks),
        (upper_inverse_hbm.at[0], upper_inverse),
    ]
    loads = [
        pltpu.make_async_copy(source, target, load_sems.at[at])
        for at, (source, target) in enumerate(pieces)
    ]
    for load in loads:
        load.start()

    barrier = pltpu.get_barrier_semaphore()
    partners = sorted({offset for plan in plans for phase in plan for offset in phase})
    for offset in partners:
        pl.semaphore_signal(
            barrier, inc=1, device_id=peer(offset), device_id_type=pl.DeviceIdType.MESH
        )

    columns = lax.broadcasted_iota(jnp.int32, (RHS, W), 1)

    def padded(slot, values):
        return jnp.where(columns < widths_ref[0, slot], values, 0.0)

    def spread(scalar):
        return jnp.full((RHS, W), scalar, jnp.int32)

    far = [spread(far_ref[0, slot]) for slot in range(LOCAL_COUNT + 1)]
    my_level = spread(owner_ref[device])

    counts = [0, 0]
    sends = []

    def exchange(values, plan, narrow):
        for phase in plan:
            outbox = counts[0]
            counts[0] += 1
            rounded = half(values)
            outgoing[outbox] = rounded
            copies = []
            for offset in phase:
                at = counts[1]
                counts[1] += 1
                copy = pltpu.make_async_remote_copy(
                    src_ref=outgoing.at[outbox],
                    dst_ref=incoming.at[at],
                    send_sem=send_sems.at[at],
                    recv_sem=recv_sems.at[at],
                    device_id=peer(offset),
                    device_id_type=pl.DeviceIdType.MESH,
                )
                copy.start()
                copies.append((copy, at))
            sends.extend(copies)
            if narrow:
                values = rounded.astype(jnp.float32)
            for copy, at in copies:
                copy.wait_recv()
                values = values + incoming[at].astype(jnp.float32)
        return values

    pending = [None] + [jnp.zeros((RHS, W), jnp.float32) for _ in range(upper_levels)]

    def scatter_up(product, slot, height):
        for level in range(1, upper_levels + 1):
            pending[level] = pending[level] + jnp.where(
                far[slot] == level + LOCAL_LEVELS - 1 - height, product, 0.0
            )

    forward = [None] * (LOCAL_COUNT + 1)
    loads[0].wait()
    loads[1].wait()
    for slot in range(2):
        forward[slot] = padded(slot, times(half(rights[slot]), lower_inverse[slot]))
    loads[2].wait()
    near = times(half(forward[0]), lower_blocks[0, 0]) + times(
        half(forward[1]), lower_blocks[1, 0]
    )
    loads[3].wait()
    loads[4].wait()
    forward[2] = padded(2, times(half(rights[2] - near), lower_inverse[2]))
    pending[1] = pending[1] + times(half(forward[2]), lower_blocks[2, 0])
    scatter_up(times(half(forward[2]), lower_blocks[2, 1]), 2, 1)
    for slot in range(2):
        scatter_up(times(half(forward[slot]), lower_blocks[slot, 1]), slot, 0)

    pl.semaphore_wait(barrier, len(partners))

    own_forward = jnp.zeros((RHS, W), jnp.float32)
    for level in range(1, upper_levels + 1):
        gathered = exchange(pending[level], plans[level - 1], False)
        solved = padded(OWN, times(half(rights[OWN] - gathered), lower_inverse[OWN]))
        solved = jnp.where(my_level == level, solved, 0.0)
        own_forward = own_forward + solved
        if level < upper_levels:
            rounded = half(solved)
            pending[level + 1] = pending[level + 1] + times(rounded, lower_blocks[OWN, 0])
            product = times(rounded, lower_blocks[OWN, 1])
            for target in range(level + 1, upper_levels + 1):
                pending[target] = pending[target] + jnp.where(
                    far[OWN] == target - level, product, 0.0
                )

    loads[5].wait()
    loads[6].wait()
    known = [None] * (upper_levels + 1)

    def pick(slot, below):
        chosen = jnp.zeros((RHS, W), jnp.float32)
        for level in range(max(1, below + 1), upper_levels + 1):
            chosen = chosen + jnp.where(far[slot] == level - below, known[level], 0.0)
        return half(chosen)

    own_solution = jnp.zeros((RHS, W), jnp.float32)
    for level in range(upper_levels, 0, -1):
        residue = own_forward
        if level < upper_levels:
            residue = residue - times(half(known[level + 1]), upper_blocks[OWN, 0])
            residue = residue - times(pick(OWN, level), upper_blocks[OWN, 1])
        solved = padded(OWN, times(half(residue), upper_inverse[OWN]))
        solved = jnp.where(my_level == level, solved, 0.0)
        own_solution = own_solution + solved
        known[level] = exchange(solved, plans[level - 1], True)
    out_ref[0, OWN] = own_solution

    residue = forward[2] - times(pick(2, 0), upper_blocks[2, 1])
    residue = residue - times(half(known[1]), upper_blocks[2, 0])
    root = padded(2, times(half(residue), upper_inverse[2]))
    out_ref[0, 2] = root
    for slot in range(2):
        residue = forward[slot] - times(pick(slot, -1), upper_blocks[slot, 1])
        residue = residue - times(half(root), upper_blocks[slot, 0])
        out_ref[0, slot] = padded(slot, times(half(residue), upper_inverse[slot]))

    for copy, _ in sends:
        copy.wait_send()


def local(
    spans,
    right_sides,
    lower_inverse,
    upper_inverse,
    lower_blocks,
    upper_blocks,
    node_widths,
    far_levels,
    owner_level,
):
    layer_span, row_span, col_span = spans
    col_levels = col_span.bit_length() - 1
    upper_levels = (layer_span * row_span * col_span).bit_length() - 1
    plans = [exchange_plan(level, col_levels) for level in range(1, upper_levels + 1)]
    phases = 2 * sum(len(plan) for plan in plans)
    messages = 2 * sum(len(phase) for plan in plans for phase in plan)
    hbm = pl.BlockSpec(memory_space=pl.ANY)
    smem = pl.BlockSpec(memory_space=pltpu.SMEM)
    return pl.pallas_call(
        functools.partial(kernel, spans, plans),
        out_shape=jax.ShapeDtypeStruct(right_sides.shape, jnp.float32),
        in_specs=[hbm] * 5 + [smem] * 3,
        out_specs=pl.BlockSpec(memory_space=pltpu.VMEM),
        scratch_shapes=[
            pltpu.VMEM(right_sides.shape[1:], jnp.float32),
            pltpu.VMEM(lower_inverse.shape[1:], jnp.bfloat16),
            pltpu.VMEM(upper_inverse.shape[1:], jnp.bfloat16),
            pltpu.VMEM(lower_blocks.shape[1:], jnp.bfloat16),
            pltpu.VMEM(upper_blocks.shape[1:], jnp.bfloat16),
            pltpu.VMEM((phases, RHS, W), jnp.bfloat16),
            pltpu.VMEM((messages, RHS, W), jnp.bfloat16),
            pltpu.SemaphoreType.DMA((7,)),
            pltpu.SemaphoreType.DMA((messages,)),
            pltpu.SemaphoreType.DMA((messages,)),
        ],
        compiler_params=pltpu.CompilerParams(collective_id=0, has_side_effects=True),
        name="tree_solve",
    )(
        right_sides,
        lower_inverse,
        upper_inverse,
        lower_blocks,
        upper_blocks,
        node_widths,
        far_levels,
        owner_level,
    )


def solution(mesh):
    spans = tuple(mesh.shape[axis] for axis in AXES)
    split = P(AXES)
    return jax.shard_map(
        functools.partial(local, spans),
        mesh=mesh,
        in_specs=(split,) * 7 + (P(),),
        out_specs=split,
        check_vma=False,
    )
```

time: 454 us -> 64.8 us (0.14)
  blocking collectives: 429 us -> 0 us
  Pallas kernels: 0 us -> 63.2 us
  matrix products: 9.61 us -> 0 us
  between operations: 9.28 us -> 0.01 us
    psum x10 -> x0, blocking collectives: 429 us -> none  [the longest x2 148 us: group_share(): lax.psum(spread_slots(partial_value, grid_span // 2 ** height, slot_at),...]
    pallas_call x0 -> x1, Pallas kernels: none -> 63.2 us  [local(): pl.pallas_call(functools.partial(kernel, spans, plans), out_shape=jax.Sha...]
    dot_general x32 -> x0, matrix products: 9.61 us -> none  [the longest x9 5.01 us: apply_blocks(): jnp.einsum('snrk,snak->snra', vectors, blocks, preferred_element_type=jnp...]
where the time goes in v1:
time: 64.8 us; the launch traced here: 64.7 us
  Pallas kernels  63.2 us (98%)
  local copies, waits for them, and re-layouts  1.47 us (2%)
    pallas_call x1, Pallas kernels, local(): pl.pallas_call(functools.partial(kernel, spans, plans), out_shape=jax.Sha...  63.2 us
    unnamed x1, local copies, waits for them, and re-layouts  1.47 us

profile of v1, /device:TPU:0, one launch (start us, length us, event | category | flops | bytes accessed | tf_op | source)
XLA Modules:
  0.0 64.7 jit_solution(1358934986875624233)
XLA Ops:
  0.0 63.2 %tree_solve.1 = f32[1,4,16,256]{3,2,1,0:T(8,128)} custom-call(f32[1,4,16,256]{3,2,1,0:T(8,128)} %rights_hbm.1, bf16[1,4,256,256]{3,2,1,0:T(8,128)(2,1)} %lower_inverse_hbm.1, bf16[1,4,256,256]{3,2,1,0:T(8,128)(2,1)} %upper_inverse_hbm.1, bf16[1,4,2,256,256]{4,3,2,1,0:T(8,128)(2,1)} %lower_blocks_hbm.1, bf16[1,4,2,256,256]{4,3,2,1,0:T(8,128)(2,1)} %upper_blocks_hbm.1, ...), custom_call_target="tpu_custom_call" | custom-call | tf_op jit(solution)/shard_map/tree_solve/pallas_call | solution.py:247
  63.2 1.5 %copy.10 = f32[1,4,16,256]{3,2,1,0:T(8,128)} copy(f32[1,4,16,256]{3,2,1,0:T(8,128)} %tree_solve.1) | data formatting | bytes 131072

commit v2 on v1

--- a/solution.py
+++ b/solution.py
@@ -30,8 +30,8 @@
     phases = []
     low = 0
     while low < level:
-        high = min(low + 2, col_levels, level) if low < col_levels else min(low + 3, level)
-        phases.append([step << low for step in range(1, 1 << (high - low))])
+        high = min(low + 4, level)
+        phases.append([step << low for step in range((1 << (high - low)) - 1, 0, -1)])
         low = high
     return phases
 
@@ -65,6 +65,7 @@
     upper_blocks,
     outgoing,
     incoming,
+    fused,
     load_sems,
     send_sems,
     recv_sems,
@@ -108,39 +109,47 @@
 
     columns = lax.broadcasted_iota(jnp.int32, (RHS, W), 1)
 
-    def padded(slot, values):
-        return jnp.where(columns < widths_ref[0, slot], values, 0.0)
-
     def spread(scalar):
         return jnp.full((RHS, W), scalar, jnp.int32)
 
+    inside = [columns < widths_ref[0, slot] for slot in range(LOCAL_COUNT + 1)]
     far = [spread(far_ref[0, slot]) for slot in range(LOCAL_COUNT + 1)]
     my_level = spread(owner_ref[device])
+    zeros = jnp.zeros((RHS, W), jnp.float32)
+
+    def padded(slot, values):
+        return jnp.where(inside[slot], values, 0.0)
 
     counts = [0, 0]
     sends = []
 
-    def exchange(values, plan, narrow):
-        for phase in plan:
-            outbox = counts[0]
-            counts[0] += 1
+    def launch(rounded, phase):
+        outbox = counts[0]
+        counts[0] += 1
+        outgoing[outbox] = rounded
+        copies = []
+        for offset in phase:
+            at = counts[1]
+            counts[1] += 1
+            copy = pltpu.make_async_remote_copy(
+                src_ref=outgoing.at[outbox],
+                dst_ref=incoming.at[at],
+                send_sem=send_sems.at[at],
+                recv_sem=recv_sems.at[at],
+                device_id=peer(offset),
+                device_id_type=pl.DeviceIdType.MESH,
+            )
+            copy.start()
+            copies.append((copy, at))
+        sends.extend(copies)
+        return copies
+
+    def exchange(values, plan, narrow, beside):
+        for index, phase in enumerate(plan):
             rounded = half(values)
-            outgoing[outbox] = rounded
-            copies = []
-            for offset in phase:
-                at = counts[1]
-                counts[1] += 1
-                copy = pltpu.make_async_remote_copy(
-                    src_ref=outgoing.at[outbox],
-                    dst_ref=incoming.at[at],
-                    send_sem=send_sems.at[at],
-                    recv_sem=recv_sems.at[at],
-                    device_id=peer(offset),
-                    device_id_type=pl.DeviceIdType.MESH,
-                )
-                copy.start()
-                copies.append((copy, at))
-            sends.extend(copies)
+            copies = launch(rounded, phase)
+            if index == 0:
+                beside()
             if narrow:
                 values = rounded.astype(jnp.float32)
             for copy, at in copies:
@@ -148,7 +157,7 @@
                 values = values + incoming[at].astype(jnp.float32)
         return values
 
-    pending = [None] + [jnp.zeros((RHS, W), jnp.float32) for _ in range(upper_levels)]
+    pending = [None] + [zeros for _ in range(upper_levels)]
 
     def scatter_up(product, slot, height):
         for level in range(1, upper_levels + 1):
@@ -165,61 +174,121 @@
     near = times(half(forward[0]), lower_blocks[0, 0]) + times(
         half(forward[1]), lower_blocks[1, 0]
     )
+    for slot in range(2):
+        scatter_up(times(half(forward[slot]), lower_blocks[slot, 1]), slot, 0)
     loads[3].wait()
     loads[4].wait()
     forward[2] = padded(2, times(half(rights[2] - near), lower_inverse[2]))
     pending[1] = pending[1] + times(half(forward[2]), lower_blocks[2, 0])
     scatter_up(times(half(forward[2]), lower_blocks[2, 1]), 2, 1)
-    for slot in range(2):
-        scatter_up(times(half(forward[slot]), lower_blocks[slot, 1]), slot, 0)
 
     pl.semaphore_wait(barrier, len(partners))
 
-    own_forward = jnp.zeros((RHS, W), jnp.float32)
+    wide_columns = lax.broadcasted_iota(jnp.int32, (W, W), 1)
+
+    def lower_product(block_id):
+        kept = jnp.where(
+            wide_columns < widths_ref[0, OWN],
+            lower_blocks[OWN, block_id].astype(jnp.float32),
+            0.0,
+        )
+        return jnp.dot(half(kept), lower_inverse[OWN], preferred_element_type=jnp.float32)
+
+    def upper_product(slot, block_id):
+        return jnp.dot(
+            upper_inverse[slot], upper_blocks[slot, block_id], preferred_element_type=jnp.float32
+        )
+
+    def split_times(values, matrix):
+        large = half(values)
+        small = half(values - large.astype(jnp.float32))
+        return times(large, matrix) + times(small, matrix)
+
+    far_is_near = jnp.full((W, W), far_ref[0, OWN], jnp.int32) == 1
+
+    own_forward = [zeros]
+    residue = [None]
+
+    def own_solve(level):
+        solved = padded(OWN, times(residue[0], lower_inverse[OWN]))
+        own_forward[0] = own_forward[0] + jnp.where(my_level == level, solved, 0.0)
+
+    def far_up(level):
+        product = jnp.where(my_level == level, times(residue[0], fused[1]), 0.0)
+        for target in range(level + 2, upper_levels + 1):
+            pending[target] = pending[target] + jnp.where(
+                far[OWN] == target - level, product, 0.0
+            )
+
+    def beside_up(level):
+        if level == 1:
+            far_product = lower_product(1)
+            fused[1] = half(far_product)
+            fused[0] = half(lower_product(0) + jnp.where(far_is_near, far_product, 0.0))
+        else:
+            far_up(level - 1)
+            own_solve(level - 1)
+        if level == 2:
+            loads[5].wait()
+            loads[6].wait()
+            far_product = upper_product(OWN, 1)
+            fused[3] = half(far_product)
+            fused[2] = half(upper_product(OWN, 0) + jnp.where(far_is_near, far_product, 0.0))
+        if 3 <= level < 3 + LOCAL_COUNT:
+            slot = level - 3
+            for block_id in range(NB):
+                fused[4 + 2 * slot + block_id] = half(upper_product(slot, block_id))
+
     for level in range(1, upper_levels + 1):
-        gathered = exchange(pending[level], plans[level - 1], False)
-        solved = padded(OWN, times(half(rights[OWN] - gathered), lower_inverse[OWN]))
-        solved = jnp.where(my_level == level, solved, 0.0)
-        own_forward = own_forward + solved
+        gathered = exchange(
+            pending[level], plans[level - 1], False, functools.partial(beside_up, level)
+        )
+        residue[0] = half(rights[OWN] - gathered)
         if level < upper_levels:
-            rounded = half(solved)
-            pending[level + 1] = pending[level + 1] + times(rounded, lower_blocks[OWN, 0])
-            product = times(rounded, lower_blocks[OWN, 1])
-            for target in range(level + 1, upper_levels + 1):
-                pending[target] = pending[target] + jnp.where(
-                    far[OWN] == target - level, product, 0.0
-                )
-
-    loads[5].wait()
-    loads[6].wait()
+            product = times(residue[0], fused[0])
+            pending[level + 1] = pending[level + 1] + jnp.where(my_level == level, product, 0.0)
+    own_solve(upper_levels)
+
     known = [None] * (upper_levels + 1)
 
-    def pick(slot, below):
-        chosen = jnp.zeros((RHS, W), jnp.float32)
-        for level in range(max(1, below + 1), upper_levels + 1):
+    def pick(slot, below, lowest):
+        chosen = zeros
+        for level in range(lowest, upper_levels + 1):
             chosen = chosen + jnp.where(far[slot] == level - below, known[level], 0.0)
         return half(chosen)
 
-    own_solution = jnp.zeros((RHS, W), jnp.float32)
+    base = [split_times(own_forward[0], upper_inverse[OWN])]
+    own_solution = zeros
+    leaf_base = [None] * LOCAL_COUNT
+    far_part = [zeros]
+
+    def beside_down(level):
+        if level == upper_levels:
+            for slot in range(LOCAL_COUNT):
+                leaf_base[slot] = split_times(forward[slot], upper_inverse[slot])
+        if 1 < level < upper_levels:
+            far_part[0] = times(pick(OWN, level - 1, level + 1), fused[3])
+        if level == 1 and upper_levels > 1:
+            leaf_base[2] = leaf_base[2] - times(pick(2, 0, 2), fused[4 + 2 * 2 + 1])
+
     for level in range(upper_levels, 0, -1):
-        residue = own_forward
+        solved = base[0]
         if level < upper_levels:
-            residue = residue - times(half(known[level + 1]), upper_blocks[OWN, 0])
-            residue = residue - times(pick(OWN, level), upper_blocks[OWN, 1])
-        solved = padded(OWN, times(half(residue), upper_inverse[OWN]))
-        solved = jnp.where(my_level == level, solved, 0.0)
+            solved = solved - far_part[0] - times(half(known[level + 1]), fused[2])
+        solved = jnp.where((my_level == level) & inside[OWN], solved, 0.0)
         own_solution = own_solution + solved
-        known[level] = exchange(solved, plans[level - 1], True)
+        known[level] = exchange(
+            solved, plans[level - 1], True, functools.partial(beside_down, level)
+        )
     out_ref[0, OWN] = own_solution
 
-    residue = forward[2] - times(pick(2, 0), upper_blocks[2, 1])
-    residue = residue - times(half(known[1]), upper_blocks[2, 0])
-    root = padded(2, times(half(residue), upper_inverse[2]))
+    nearest = half(known[1])
+    root = padded(2, leaf_base[2] - times(nearest, fused[4 + 2 * 2]))
     out_ref[0, 2] = root
     for slot in range(2):
-        residue = forward[slot] - times(pick(slot, -1), upper_blocks[slot, 1])
-        residue = residue - times(half(root), upper_blocks[slot, 0])
-        out_ref[0, slot] = padded(slot, times(half(residue), upper_inverse[slot]))
+        solved = leaf_base[slot] - times(pick(slot, -1, 1), fused[4 + 2 * slot + 1])
+        solved = solved - times(half(root), fused[4 + 2 * slot])
+        out_ref[0, slot] = padded(slot, solved)
 
     for copy, _ in sends:
         copy.wait_send()
@@ -257,6 +326,7 @@
             pltpu.VMEM(upper_blocks.shape[1:], jnp.bfloat16),
             pltpu.VMEM((phases, RHS, W), jnp.bfloat16),
             pltpu.VMEM((messages, RHS, W), jnp.bfloat16),
+            pltpu.VMEM((4 + NB * LOCAL_COUNT, W, W), jnp.bfloat16),
             pltpu.SemaphoreType.DMA((7,)),
             pltpu.SemaphoreType.DMA((messages,)),
             pltpu.SemaphoreType.DMA((messages,)),

time: 64.8 us -> 54.4 us (0.84)
  Pallas kernels: 63.2 us -> 52.8 us
    pallas_call x1, Pallas kernels: 63.2 us -> 52.8 us  [local(): pl.pallas_call(functools.partial(kernel, spans, plans), out_shape=jax.Sha...]
where the time goes in v2:
time: 54.4 us; the launch traced here: 54.3 us
  Pallas kernels  52.8 us (97%)
  local copies, waits for them, and re-layouts  1.47 us (3%)
    pallas_call x1, Pallas kernels, local(): pl.pallas_call(functools.partial(kernel, spans, plans), out_shape=jax.Sha...  52.8 us
    unnamed x1, local copies, waits for them, and re-layouts  1.47 us

profile of v2, /device:TPU:0, one launch (start us, length us, event | category | flops | bytes accessed | tf_op | source)
XLA Modules:
  0.0 54.3 jit_solution(14306311777891894200)
XLA Ops:
  0.0 52.8 %tree_solve.1 = f32[1,4,16,256]{3,2,1,0:T(8,128)} custom-call(f32[1,4,16,256]{3,2,1,0:T(8,128)} %rights_hbm.1, bf16[1,4,256,256]{3,2,1,0:T(8,128)(2,1)} %lower_inverse_hbm.1, bf16[1,4,256,256]{3,2,1,0:T(8,128)(2,1)} %upper_inverse_hbm.1, bf16[1,4,2,256,256]{4,3,2,1,0:T(8,128)(2,1)} %lower_blocks_hbm.1, bf16[1,4,2,256,256]{4,3,2,1,0:T(8,128)(2,1)} %upper_blocks_hbm.1, ...), custom_call_target="tpu_custom_call" | custom-call | tf_op jit(solution)/shard_map/tree_solve/pallas_call | solution.py:316
  52.8 1.5 %copy.10 = f32[1,4,16,256]{3,2,1,0:T(8,128)} copy(f32[1,4,16,256]{3,2,1,0:T(8,128)} %tree_solve.1) | data formatting | bytes 131072

commit v3 on v2

--- a/solution.py
+++ b/solution.py
@@ -26,9 +26,8 @@
     return flipped
 
 
-def exchange_plan(level, col_levels):
+def exchange_plan(level, low=0):
     phases = []
-    low = 0
     while low < level:
         high = min(low + 4, level)
         phases.append([step << low for step in range((1 << (high - low)) - 1, 0, -1)])
@@ -46,9 +45,20 @@
     return values.astype(jnp.bfloat16)
 
 
+HANDOUT = {
+    2: ((1, False, 0),),
+    3: ((2, False, 0),(1, False, 1)),
+    4: ((2, False, 1),(1, True, 0)),
+    5: ((1, True, 1),),
+}
+NEAR_BITS = 2
+NEAR = 2**NEAR_BITS
+
+
 def kernel(
     spans,
     plans,
+    down_plans,
     rights_hbm,
     lower_inverse_hbm,
     upper_inverse_hbm,
@@ -66,9 +76,14 @@
     outgoing,
     incoming,
     fused,
+    replicas,
+    fars,
+    bases,
     load_sems,
     send_sems,
     recv_sems,
+    bulk_send_sems,
+    bulk_recv_sems,
 ):
     layer_span, row_span, col_span = spans
     upper_levels = len(plans)
@@ -144,6 +159,27 @@
         sends.extend(copies)
         return copies
 
+    bulk = {}
+
+    def hand_out(name, source, target, offset):
+        at = len(bulk)
+        bulk[name] = pltpu.make_async_remote_copy(
+            src_ref=source,
+            dst_ref=target,
+            send_sem=bulk_send_sems.at[at],
+            recv_sem=bulk_recv_sems.at[at],
+            device_id=peer(offset),
+            device_id_type=pl.DeviceIdType.MESH,
+        )
+        bulk[name].start()
+
+    received = set()
+
+    def await_bulk(name):
+        if name not in received:
+            received.add(name)
+            bulk[name].wait_recv()
+
     def exchange(values, plan, narrow, beside):
         for index, phase in enumerate(plan):
             rounded = half(values)
@@ -220,20 +256,43 @@
                 far[OWN] == target - level, product, 0.0
             )
 
+    wide_rows = lax.broadcasted_iota(jnp.int32, (W, W), 0)
+
+    def upper_kept(block_id):
+        return jnp.where(
+            wide_rows < widths_ref[0, OWN], upper_product(OWN, block_id), 0.0
+        )
+
     def beside_up(level):
         if level == 1:
+            fars[0] = far[OWN].astype(jnp.float32)
+            for offset in range(1, NEAR):
+                hand_out(("far", offset), fars.at[0], fars.at[offset], offset)
             far_product = lower_product(1)
             fused[1] = half(far_product)
             fused[0] = half(lower_product(0) + jnp.where(far_is_near, far_product, 0.0))
+            loads[5].wait()
+            loads[6].wait()
+            far_product = upper_kept(1)
+            replicas[0, 1] = half(far_product)
+            replicas[0, 0] = half(upper_kept(0) + jnp.where(far_is_near, far_product, 0.0))
         else:
             far_up(level - 1)
             own_solve(level - 1)
-        if level == 2:
-            loads[5].wait()
-            loads[6].wait()
-            far_product = upper_product(OWN, 1)
-            fused[3] = half(far_product)
-            fused[2] = half(upper_product(OWN, 0) + jnp.where(far_is_near, far_product, 0.0))
+        if level == upper_levels:
+            bases[0] = padded(OWN, split_times(own_forward[0], upper_inverse[OWN]))
+            for offset in reversed(range(1, NEAR)):
+                hand_out(("base", offset), bases.at[0], bases.at[offset], offset)
+        for offset, relayed, block_id in HANDOUT.get(level, ()):
+            kept = 2 if relayed else 0
+            if relayed:
+                await_bulk((2, False, block_id))
+            hand_out(
+                (offset, relayed, block_id),
+                replicas.at[kept, block_id],
+                replicas.at[kept + offset, block_id],
+                offset,
+            )
         if 3 <= level < 3 + LOCAL_COUNT:
             slot = level - 3
             for block_id in range(NB):
@@ -257,29 +316,56 @@
             chosen = chosen + jnp.where(far[slot] == level - below, known[level], 0.0)
         return half(chosen)
 
-    base = [split_times(own_forward[0], upper_inverse[OWN])]
     own_solution = zeros
     leaf_base = [None] * LOCAL_COUNT
     far_part = [zeros]
+    near_levels = [owner_ref[flip_bits(device, offset)] for offset in range(NEAR)]
+
+    def holder(level):
+        offset_of = jnp.int32(0)
+        found = jnp.int32(0)
+        for offset in range(min(NEAR, 2**level)):
+            offset_of = jnp.where(near_levels[offset] == level, offset, offset_of)
+            found = jnp.where(near_levels[offset] == level, 1, found)
+        return offset_of, found
+
+    def prepare(level):
+        if level < 1 or level + 2 > upper_levels:
+            return
+        at, _ = holder(level)
+        reach = fars[at]
+        chosen = zeros
+        for target in range(level + 2, upper_levels + 1):
+            chosen = chosen + jnp.where(reach == float(target - level), known[target], 0.0)
+        far_part[0] = times(half(chosen), replicas[at, 1])
 
     def beside_down(level):
         if level == upper_levels:
             for slot in range(LOCAL_COUNT):
                 leaf_base[slot] = split_times(forward[slot], upper_inverse[slot])
-        if 1 < level < upper_levels:
-            far_part[0] = times(pick(OWN, level - 1, level + 1), fused[3])
-        if level == 1 and upper_levels > 1:
-            leaf_base[2] = leaf_base[2] - times(pick(2, 0, 2), fused[4 + 2 * 2 + 1])
+        else:
+            prepare(level - 1)
 
     for level in range(upper_levels, 0, -1):
-        solved = base[0]
-        if level < upper_levels:
-            solved = solved - far_part[0] - times(half(known[level + 1]), fused[2])
-        solved = jnp.where((my_level == level) & inside[OWN], solved, 0.0)
-        own_solution = own_solution + solved
-        known[level] = exchange(
-            solved, plans[level - 1], True, functools.partial(beside_down, level)
-        )
+        if level == upper_levels:
+            solved = padded(OWN, split_times(own_forward[0], upper_inverse[OWN]))
+            solved = jnp.where(my_level == level, solved, 0.0)
+        else:
+            at, found = holder(level)
+            solved = bases[at] - far_part[0] - times(half(known[level + 1]), replicas[at, 0])
+            solved = jnp.where(spread(found) == 1, solved, 0.0)
+        own_solution = own_solution + jnp.where(my_level == level, solved, 0.0)
+        if down_plans[level - 1]:
+            known[level] = exchange(
+                solved, down_plans[level - 1], True, functools.partial(beside_down, level)
+            )
+        else:
+            known[level] = half(solved).astype(jnp.float32)
+            beside_down(level)
+        if level == upper_levels:
+            for name in bulk:
+                await_bulk(name)
+    leaf_base[2] = leaf_base[2] - times(pick(2, 0, 2), fused[4 + 2 * 2 + 1])
     out_ref[0, OWN] = own_solution
 
     nearest = half(known[1])
@@ -291,6 +377,8 @@
         out_ref[0, slot] = padded(slot, solved)
 
     for copy, _ in sends:
+        copy.wait_send()
+    for copy in bulk.values():
         copy.wait_send()
 
 
@@ -306,15 +394,17 @@
     owner_level,
 ):
     layer_span, row_span, col_span = spans
-    col_levels = col_span.bit_length() - 1
     upper_levels = (layer_span * row_span * col_span).bit_length() - 1
-    plans = [exchange_plan(level, col_levels) for level in range(1, upper_levels + 1)]
-    phases = 2 * sum(len(plan) for plan in plans)
-    messages = 2 * sum(len(phase) for plan in plans for phase in plan)
+    plans = [exchange_plan(level) for level in range(1, upper_levels + 1)]
+    down_plans = [exchange_plan(level, NEAR_BITS) for level in range(1, upper_levels)]
+    down_plans.append(plans[-1])
+    phases = sum(len(plan) for plan in plans + down_plans)
+    messages = sum(len(phase) for plan in plans + down_plans for phase in plan)
+    handed = 2 * (NEAR - 1) + sum(len(row) for row in HANDOUT.values())
     hbm = pl.BlockSpec(memory_space=pl.ANY)
     smem = pl.BlockSpec(memory_space=pltpu.SMEM)
     return pl.pallas_call(
-        functools.partial(kernel, spans, plans),
+        functools.partial(kernel, spans, plans, down_plans),
         out_shape=jax.ShapeDtypeStruct(right_sides.shape, jnp.float32),
         in_specs=[hbm] * 5 + [smem] * 3,
         out_specs=pl.BlockSpec(memory_space=pltpu.VMEM),
@@ -327,9 +417,14 @@
             pltpu.VMEM((phases, RHS, W), jnp.bfloat16),
             pltpu.VMEM((messages, RHS, W), jnp.bfloat16),
             pltpu.VMEM((4 + NB * LOCAL_COUNT, W, W), jnp.bfloat16),
+            pltpu.VMEM((NEAR, NB, W, W), jnp.bfloat16),
+            pltpu.VMEM((NEAR, RHS, W), jnp.float32),
+            pltpu.VMEM((NEAR, RHS, W), jnp.float32),
             pltpu.SemaphoreType.DMA((7,)),
             pltpu.SemaphoreType.DMA((messages,)),
             pltpu.SemaphoreType.DMA((messages,)),
+            pltpu.SemaphoreType.DMA((handed,)),
+            pltpu.SemaphoreType.DMA((handed,)),
         ],
         compiler_params=pltpu.CompilerParams(collective_id=0, has_side_effects=True),
         name="tree_solve",

time: 54.4 us -> 50.2 us (0.923)
  Pallas kernels: 52.8 us -> 48.5 us
    pallas_call x1, Pallas kernels: 52.8 us -> 48.5 us  [local(): pl.pallas_call(functools.partial(kernel, spans, plans, down_plans), out_s...]
where the time goes in v3:
time: 50.2 us; the launch traced here: 50 us
  Pallas kernels  48.5 us (97%)
  local copies, waits for them, and re-layouts  1.47 us (3%)
    pallas_call x1, Pallas kernels, local(): pl.pallas_call(functools.partial(kernel, spans, plans, down_plans), out_s...  48.5 us
    unnamed x1, local copies, waits for them, and re-layouts  1.47 us

profile of v3, /device:TPU:0, one launch (start us, length us, event | category | flops | bytes accessed | tf_op | source)
XLA Modules:
  0.0 50.0 jit_solution(17770108806762481978)
XLA Ops:
  0.0 48.5 %tree_solve.1 = f32[1,4,16,256]{3,2,1,0:T(8,128)} custom-call(f32[1,4,16,256]{3,2,1,0:T(8,128)} %rights_hbm.1, bf16[1,4,256,256]{3,2,1,0:T(8,128)(2,1)} %lower_inverse_hbm.1, bf16[1,4,256,256]{3,2,1,0:T(8,128)(2,1)} %upper_inverse_hbm.1, bf16[1,4,2,256,256]{4,3,2,1,0:T(8,128)(2,1)} %lower_blocks_hbm.1, bf16[1,4,2,256,256]{4,3,2,1,0:T(8,128)(2,1)} %upper_blocks_hbm.1, ...), custom_call_target="tpu_custom_call" | custom-call | tf_op jit(solution)/shard_map/tree_solve/pallas_call | solution.py:406
  48.5 1.5 %copy.10 = f32[1,4,16,256]{3,2,1,0:T(8,128)} copy(f32[1,4,16,256]{3,2,1,0:T(8,128)} %tree_solve.1) | data formatting | bytes 131072
